TPU v7x, 32 devices: a whole 2x2x4 slice. The times are simulated.
32 devices in a mesh: dp: 2 (over y), expert: 4 (over z), tile: 4 (over x, core).
Axes of the slice: x: 2, y: 2, z: 4, core: 2. Of those that a mesh axis runs over, the one named last changes fastest.
Arguments:
- tokens: bfloat16 [512, 4096], P(('dp', 'expert'), 'tile'), may hold values from -6 to 6
- hidden: bfloat16 [512, 2, 7168], P(('dp', 'expert'), None, 'tile'), may hold values from -6 to 6
- routes: int32 [512, 2], P(('dp', 'expert')), may hold values from 0 to 3, all different within a row; in each aligned block of 64 rows (0 to 63, 64 to 127, ...) at most 40 rows name the same one
- lengths: int32 [8], P(('dp', 'expert')), may hold values from 1 to 64, as said below
Outputs:
- hessian_in: float32 [4, 4096, 4096], P('expert', 'tile', 'dp')
- hessian_down: float32 [4, 7168, 7168], P('expert', 'tile', 'dp')
Inputs may be any that keep to these rules, and one draw needn't show every extreme that they name: `routes`: in each aligned block of 64 rows (the rows of one group) no expert is named by more than 40 rows, a bound that some block reaches. The live rows of group g are its first lengths[g] rows; the last group is full.
All inputs are finite; a program needn't handle non-finite values.
Results may differ from a plain program's by a relative error of at most 0.0003.
Values may be sent and summed in bfloat16 or wider, within the bound.
No kernel may reach another device: no remote copies, remote signals or barrier semaphores. Data moves between devices by JAX's collectives and lax.ppermute only.
A program may use at most 128 MiB of HBM per device.

v0:
```python
import jax
import jax.numpy as jnp
from jax import lax
from jax.sharding import PartitionSpec as P


def broadcast(value, axis, source):
    kept = jnp.where(lax.axis_index(axis) == source, value, 0).astype(value.dtype)
    return lax.psum(kept, axis)


def contract(left, right):
    return lax.dot_general(
        left, right, (((0,), (0,)), ((), ())), preferred_element_type=jnp.float32
    )


def dispatch_tables(routes, live_count, experts, share_size, senders):
    token_count = routes.shape[0]
    top_count = routes.shape[1]
    flat_routes = routes.reshape(token_count * top_count)
    pair_index = jnp.arange(token_count * top_count, dtype=jnp.int32)
    pair_live = pair_index // top_count < live_count
    expert_ids = jnp.arange(experts, dtype=jnp.int32)
    onehot = ((flat_routes[:, None] == expert_ids[None, :]) & pair_live[:, None]).astype(
        jnp.float32
    )
    before = jnp.cumsum(onehot, axis=0) - onehot
    position = jnp.sum(before * onehot, axis=1).astype(jnp.int32)
    target = (
        position // share_size * (experts * share_size)
        + flat_routes * share_size
        + position % share_size
    )
    slot_total = senders * experts * share_size
    placed = (target[None, :] == jnp.arange(slot_total, dtype=jnp.int32)[:, None]) & pair_live[
        None, :
    ]
    return (placed.astype(jnp.float32), jnp.sum(onehot, axis=0))


def on_device(tokens, hidden, routes, lengths):
    experts = lax.axis_size("expert")
    senders = lax.axis_size("dp")
    tiles = lax.axis_size("tile")
    token_count = tokens.shape[0]
    top_count = routes.shape[1]
    share_size = (5 * token_count + 2 * experts * senders - 1) // (2 * experts * senders)
    placed, local_counts = dispatch_tables(routes, lengths[0], experts, share_size, senders)
    slot_total = placed.shape[0]
    by_token = jnp.sum(placed.reshape(slot_total, token_count, top_count), axis=2).astype(
        jnp.bfloat16
    )
    send_tokens = jnp.dot(by_token, tokens, preferred_element_type=jnp.float32).astype(jnp.bfloat16)
    flat_hidden = hidden.reshape(token_count * top_count, hidden.shape[2])
    send_hidden = jnp.dot(
        placed.astype(jnp.bfloat16), flat_hidden, preferred_element_type=jnp.float32
    ).astype(jnp.bfloat16)
    slot_tokens, slot_hidden = (
        lax.all_to_all(send_tokens, ("dp", "expert"), split_axis=0, concat_axis=0, tiled=True),
        lax.all_to_all(send_hidden, ("dp", "expert"), split_axis=0, concat_axis=0, tiled=True),
    )
    global_counts = lax.psum(local_counts, ("dp", "expert"))
    own_expert = lax.axis_index("expert")
    own_count = jnp.sum(
        jnp.where(jnp.arange(experts, dtype=jnp.int32) == own_expert, global_counts, 0.0)
    )
    factor = 2.0 / jnp.maximum(own_count, 1.0)
    all_tokens, all_hidden = (
        lax.all_gather(slot_tokens, "dp", axis=0, tiled=True),
        lax.all_gather(slot_hidden, "dp", axis=0, tiled=True),
    )
    width_tokens = slot_tokens.shape[1] * tiles // senders
    width_hidden = slot_hidden.shape[1] * tiles // senders
    group_index = lax.axis_index("dp")
    if senders % tiles == 0:
        source_tile = group_index * tiles // senders
        offset_tokens = group_index * width_tokens - source_tile * slot_tokens.shape[1]
        offset_hidden = group_index * width_hidden - source_tile * slot_hidden.shape[1]
        own_tokens = lax.dynamic_slice_in_dim(all_tokens, offset_tokens, width_tokens, 1)
        own_hidden = lax.dynamic_slice_in_dim(all_hidden, offset_hidden, width_hidden, 1)
        joined = jnp.concatenate([own_tokens, own_hidden], axis=1)
        arrived = broadcast(joined, "tile", source_tile)
        column_tokens = arrived[:, :width_tokens]
        column_hidden = arrived[:, width_tokens:]
    else:
        wide_tokens, wide_hidden = (
            lax.all_gather(all_tokens, "tile", axis=1, tiled=True),
            lax.all_gather(all_hidden, "tile", axis=1, tiled=True),
        )
        column_tokens = lax.dynamic_slice_in_dim(
            wide_tokens, group_index * width_tokens, width_tokens, 1
        )
        column_hidden = lax.dynamic_slice_in_dim(
            wide_hidden, group_index * width_hidden, width_hidden, 1
        )
    gram_tokens = contract(all_tokens, column_tokens)
    gram_hidden = contract(all_hidden, column_hidden)
    return ((gram_tokens * factor)[None], (gram_hidden * factor)[None])


def solution(mesh):
    placed = (
        P(("dp", "expert"), "tile"),
        P(("dp", "expert"), None, "tile"),
        P(("dp", "expert"), None),
        P(("dp", "expert")),
    )
    return jax.shard_map(
        on_device,
        mesh=mesh,
        in_specs=placed,
        out_specs=(P("expert", "tile", "dp"), P("expert", "tile", "dp")),
        check_vma=False,
    )
```

profile of v0, /device:TPU:0, one launch (start us, length us, event | category | flops | bytes accessed | tf_op | source)
XLA Modules:
  0.0 152.8 jit_solution(17547992000557333005)
XLA Ops:
  7.2 0.0 copy-start
  7.2 0.0 copy-start.2
  7.9 0.8 copy.20
  8.7 0.1 eq.43
  8.8 0.1 fusion.5
  8.9 0.2 reduce_window_sum.11
  9.1 0.2 fusion.6
  9.3 1.2 reshape.90
  10.5 0.3 convolution_convert_fusion
  10.8 1.0 all_to_all.19
  11.8 7.3 %all-to-all-start.1 = ((bf16[8,20,1792]{2,1,0:T(8,128)(2,1)}), bf16[8,20,1792]{2,1,0:T(8,128)(2,1)S(1)}, u32[]{:S(2)}, u32[]{:S(2)}) async-start(bf16[8,20,1792]{2,1,0:T(8,128)(2,1)} %all_to_all.19), calls=%async_computation.1 | async-start | bytes 1376256 | tf_op jit(solution)/shard_map/all_to_all | solution.py:61
  19.1 0.0 all-gather.6.cloned.1.call-start
  19.1 0.1 ne.82
  19.3 0.1 copy.22
  19.4 0.1 div.25
  19.5 0.1 copy.23
  19.6 0.1 rem.32
  19.8 0.1 copy.21
  19.8 0.0 copy-done.2
  19.9 18.1 %all-to-all-done.1 = bf16[8,20,1792]{2,1,0:T(8,128)(2,1)S(1)} async-done(((bf16[8,20,1792]{2,1,0:T(8,128)(2,1)}), bf16[8,20,1792]{2,1,0:T(8,128)(2,1)S(1)}, u32[]{:S(2)}, u32[]{:S(2)}) %all-to-all-start.1) | async-done | bytes 573472 | tf_op jit(solution)/shard_map/all_to_all | solution.py:61
  38.0 0.9 all_to_all.21
  38.9 0.0 all-gather.6.cloned.1.call-update
  38.9 0.0 all-gather.4.cloned.1.call-start
  39.0 0.1 convert_reduce_fusion
  39.1 0.0 copy-done
  39.1 0.3 convolution_convert_fusion.1
  39.4 0.1 all_to_all.16
  39.5 14.5 %all_to_all.24 = bf16[8,20,1024]{2,1,0:T(8,128)(2,1)S(1)} all-to-all(bf16[8,20,1024]{2,1,0:T(8,128)(2,1)S(1)} %all_to_all.16), channel_id=1, replica_groups=mesh['dp'=2,'expert'=4,'tile'=4] {'dp','expert'}, dimensions={0} | all-to-all | bytes 655360 | tf_op jit(solution)/shard_map/all_to_all | solution.py:60
  54.0 0.1 all_to_all.18
  54.1 14.2 %all_gather.12 = bf16[320,1024]{1,0:T(8,128)(2,1)} all-gather(bf16[160,1024]{1,0:T(8,128)(2,1)S(1)} %all_to_all.18), channel_id=1, replica_groups=mesh['dp'=2,'expert'=4,'tile'=4] {'dp'}, dimensions={0}, use_global_device_ids=true | all-gather | bytes 983040 | tf_op jit(solution)/shard_map/all_gather | solution.py:70
  68.3 0.0 all-gather.4.cloned.1.call-update
  68.3 0.0 all-gather.8.cloned.1.call-start
  68.3 0.0 all-gather.6.cloned.1.call-done
  68.4 0.7 all-gather.8.cloned.1.call-update
  69.0 19.6 %psum.7 = f32[4]{0:T(128)S(1)} all-reduce(f32[4]{0:T(128)S(1)} %get-tuple-element.2), channel_id=1, replica_groups=mesh['dp'=2,'expert'=4,'tile'=4] {'dp','expert'}, use_global_device_ids=true, to_apply=%region_4.5 | all-reduce | flops 4 | bytes 32 | tf_op jit(solution)/shard_map/psum | solution.py:63
  88.6 0.6 fusion.16
  89.9 0.0 copy-start.1
  89.9 3.8 %all-gather.4.cloned.1.call-done = bf16[320,4096]{1,0:T(8,128)(2,1)} async-done(((bf16[320,1024]{1,0:T(8,128)(2,1)}), bf16[320,4096]{1,0:T(8,128)(2,1)}) %all-gather.4.cloned.1.call-update) | async-done | bytes 2621456 | tf_op jit(solution)/shard_map/all_gather | solution.py:88
  93.7 7.3 %multiply_bitcast_fusion.1 = f32[1,1024,2048]{2,1,0:T(8,128)} fusion(bf16[320,1024]{1,0:T(8,128)(2,1)} %all_gather.12, f32[]{:T(128)S(6)} %div.27, bf16[320,4096]{1,0:T(8,128)(2,1)} %all-gather.4.cloned.1.call-done, s32[]{:T(128)S(6)} %select_n.54), kind=kOutput, calls=%fused_computation.1 | convolution fusion | flops 1344274432 | bytes 10354696 | tf_op jit(solution)/shard_map/dot_general | solution.py:13
  101.0 31.0 %all-gather.8.cloned.1.call-done = bf16[320,7168]{1,0:T(8,128)(2,1)} async-done(((bf16[320,1792]{1,0:T(8,128)(2,1)}), bf16[320,7168]{1,0:T(8,128)(2,1)}) %all-gather.8.cloned.1.call-update) | async-done | bytes 4587536 | tf_op jit(solution)/shard_map/all_gather | solution.py:89
  132.0 0.0 copy-done.1
  132.0 14.3 %multiply_bitcast_fusion = f32[1,1792,3584]{2,1,0:T(8,128)} fusion(bf16[320,1792]{1,0:T(8,128)(2,1)S(1)} %copy-done.1, f32[]{:T(128)S(6)} %div.27, bf16[320,7168]{1,0:T(8,128)(2,1)} %all-gather.8.cloned.1.call-done, s32[]{:T(128)S(6)} %select_n.58), kind=kOutput, calls=%fused_computation | convolution fusion | flops 4116840448 | bytes 29130760 | tf_op jit(solution)/shard_map/dot_general | solution.py:13
  (5 shorter events, 0.1 us)
Async XLA Ops:
  7.2 31.9 %copy-start = (bf16[64,1024]{1,0:T(8,128)(2,1)S(1)}, bf16[64,1024]{1,0:T(8,128)(2,1)}, u32[]{:S(2)}) copy-start(bf16[64,1024]{1,0:T(8,128)(2,1)} %param.4) | copy-start | bytes 393220
  7.2 12.6 %copy-start.2 = (s32[64,2]{0,1:T(2,128)S(1)}, s32[64,2]{0,1:T(2,128)}, u32[]{:S(2)}) copy-start(s32[64,2]{0,1:T(2,128)} %param.6) | copy-start | bytes 1540
  11.8 26.2 %all-to-all-start.1 = ((bf16[8,20,1792]{2,1,0:T(8,128)(2,1)}), bf16[8,20,1792]{2,1,0:T(8,128)(2,1)S(1)}, u32[]{:S(2)}, u32[]{:S(2)}) async-start(bf16[8,20,1792]{2,1,0:T(8,128)(2,1)} %all_to_all.19), calls=%async_computation.1 | async-start | bytes 1376256 | tf_op jit(solution)/shard_map/all_to_all | solution.py:61
  19.1 49.3 %all-gather.6.cloned.1.call-start = ((), (), s32[]{:S(2)}) async-start(), calls=%async_computation.3 | async-start | bytes 1720320 | tf_op jit(solution)/shard_map/all_gather | solution.py:71
  38.9 54.8 %all-gather.4.cloned.1.call-start = ((), (), s32[]{:S(2)}) async-start(), calls=%async_computation.2 | async-start | bytes 3276800 | tf_op jit(solution)/shard_map/all_gather | solution.py:88
  68.3 63.7 %all-gather.8.cloned.1.call-start = ((), (), s32[]{:S(2)}) async-start(), calls=%async_computation.4 | async-start | bytes 5734400 | tf_op jit(solution)/shard_map/all_gather | solution.py:89
  89.9 42.1 %copy-start.1 = (bf16[320,1792]{1,0:T(8,128)(2,1)S(1)}, bf16[320,1792]{1,0:T(8,128)(2,1)}, u32[]{:S(2)}) copy-start(bf16[320,1792]{1,0:T(8,128)(2,1)} %all-gather.6.cloned.1.call-done) | copy-start | bytes 3440644
Sparse Core Ops, SparseCore 0:
  39.0 28.0 all-gather.5
  68.7 24.9 all-gather.3
  95.3 36.6 all-gather.7
where the time goes:
time: 153 us
  waiting for transfers between devices  53.6 us (35%)
  blocking collectives  48.3 us (32%)
  matrix products  22.1 us (14%)
  between operations  15.3 us (10%)
  starting transfers between devices  7.43 us (5%)
  local copies, waits for them, and re-layouts  4.82 us (3%)
    all_gather x1, waiting for transfers between devices, on_device(): lax.all_gather(all_hidden, 'tile', axis=1, tiled=True)  31 us
    dot_general x2, matrix products, contract(): lax.dot_general(left, right, (((0,), (0,)), ((), ())), preferred_element_...  21.6 us
    psum x1, blocking collectives, on_device(): global_counts = lax.psum(local_counts, ('dp', 'expert'))  19.6 us
    all_to_all x1, waiting for transfers between devices, on_device(): lax.all_to_all(send_hidden, ('dp', 'expert'), split_axis=0, concat_axis=0...  18.1 us
    all_to_all x1, blocking collectives, on_device(): lax.all_to_all(send_tokens, ('dp', 'expert'), split_axis=0, concat_axis=0...  14.5 us
    all_gather x1, blocking collectives, on_device(): lax.all_gather(slot_tokens, 'dp', axis=0, tiled=True)  14.2 us
    all_to_all x1, starting transfers between devices, on_device(): lax.all_to_all(send_hidden, ('dp', 'expert'), split_axis=0, concat_axis=0...  7.31 us
    all_gather x1, waiting for transfers between devices, on_device(): lax.all_gather(all_tokens, 'tile', axis=1, tiled=True)  3.79 us
  transfers between devices with their start and end apart: 4, of which 3 were waited for; matrix products, arithmetic and copies ran while one was open for 6% of the time, Pallas kernels for 0%

commit v1 on v0

--- a/solution.py
+++ b/solution.py
@@ -86,7 +86,7 @@
     else:
         wide_tokens, wide_hidden = (
             lax.all_gather(all_tokens, "tile", axis=1, tiled=True),
-            lax.all_gather(all_hidden, "tile", axis=1, tiled=True),
+            jnp.concatenate(lax.all_gather(all_hidden, "tile"), axis=1),
         )
         column_tokens = lax.dynamic_slice_in_dim(
             wide_tokens, group_index * width_tokens, width_tokens, 1

time: 153 us -> 159 us (1.039)
  local copies, waits for them, and re-layouts: 4.82 us -> 11.9 us
  matrix products: 22.1 us -> 20.5 us
    all_gather x0 -> x1, local copies, waits for them, and re-layouts: none -> 5.84 us  [on_device(): lax.all_gather(all_hidden, 'tile')]
    dot_general x2, matrix products: 21.6 us -> 19.9 us  [contract(): lax.dot_general(left, right, (((0,), (0,)), ((), ())), preferred_element_...]
where the time goes in v1:
time: 159 us; the launch traced here: 158 us
  waiting for transfers between devices  53.4 us (34%)
  blocking collectives  48.5 us (31%)
  matrix products  20.5 us (13%)
  between operations  15.3 us (10%)
  local copies, waits for them, and re-layouts  11.9 us (7%)
  starting transfers between devices  7.43 us (5%)
    all_gather x1, waiting for transfers between devices, on_device(): lax.all_gather(all_hidden, 'tile')  31 us
    dot_general x2, matrix products, contract(): lax.dot_general(left, right, (((0,), (0,)), ((), ())), preferred_element_...  19.9 us
    psum x1, blocking collectives, on_device(): global_counts = lax.psum(local_counts, ('dp', 'expert'))  19.8 us
    all_to_all x1, waiting for transfers between devices, on_device(): lax.all_to_all(send_hidden, ('dp', 'expert'), split_axis=0, concat_axis=0...  18.1 us
    all_to_all x1, blocking collectives, on_device(): lax.all_to_all(send_tokens, ('dp', 'expert'), split_axis=0, concat_axis=0...  14.5 us
    all_gather x1, blocking collectives, on_device(): lax.all_gather(slot_tokens, 'dp', axis=0, tiled=True)  14.2 us
    all_to_all x1, starting transfers between devices, on_device(): lax.all_to_all(send_hidden, ('dp', 'expert'), split_axis=0, concat_axis=0...  7.31 us
    all_gather x1, local copies, waits for them, and re-layouts, on_device(): lax.all_gather(all_hidden, 'tile')  5.84 us
  transfers between devices with their start and end apart: 4, of which 3 were waited for; matrix products, arithmetic and copies ran while one was open for 6% of the time, Pallas kernels for 0%

profile of v1, /device:TPU:0, one launch (start us, length us, event | category | flops | bytes accessed | tf_op | source)
XLA Modules:
  0.0 158.2 jit_solution(8036466624012088871)
XLA Ops:
  7.2 0.0 copy-start
  7.2 0.0 copy-start.2
  7.9 0.8 copy.22
  8.7 0.1 eq.43
  8.8 0.1 fusion.5
  8.9 0.2 reduce_window_sum.11
  9.1 0.2 fusion.6
  9.3 1.2 reshape.96
  10.5 0.3 convolution_convert_fusion
  10.8 1.0 all_to_all.19
  11.8 7.3 %all-to-all-start.1 = ((bf16[8,20,1792]{2,1,0:T(8,128)(2,1)}), bf16[8,20,1792]{2,1,0:T(8,128)(2,1)S(1)}, u32[]{:S(2)}, u32[]{:S(2)}) async-start(bf16[8,20,1792]{2,1,0:T(8,128)(2,1)} %all_to_all.19), calls=%async_computation.1 | async-start | bytes 1376256 | tf_op jit(solution)/shard_map/all_to_all | solution.py:61
  19.1 0.0 all-gather.7.cloned.1.call-start
  19.1 0.1 ne.82
  19.3 0.1 copy.24
  19.4 0.1 div.25
  19.5 0.1 copy.25
  19.6 0.1 rem.32
  19.8 0.1 copy.23
  19.8 0.0 copy-done.2
  19.9 18.1 %all-to-all-done.1 = bf16[8,20,1792]{2,1,0:T(8,128)(2,1)S(1)} async-done(((bf16[8,20,1792]{2,1,0:T(8,128)(2,1)}), bf16[8,20,1792]{2,1,0:T(8,128)(2,1)S(1)}, u32[]{:S(2)}, u32[]{:S(2)}) %all-to-all-start.1) | async-done | bytes 573472 | tf_op jit(solution)/shard_map/all_to_all | solution.py:61
  38.0 0.9 all_to_all.21
  38.9 0.0 all-gather.7.cloned.1.call-update
  38.9 0.0 all-gather.5.cloned.1.call-start
  39.0 0.1 convert_reduce_fusion
  39.1 0.0 copy-done
  39.1 0.3 convolution_convert_fusion.1
  39.4 0.1 all_to_all.16
  39.5 14.5 %all_to_all.24 = bf16[8,20,1024]{2,1,0:T(8,128)(2,1)S(1)} all-to-all(bf16[8,20,1024]{2,1,0:T(8,128)(2,1)S(1)} %all_to_all.16), channel_id=1, replica_groups=mesh['dp'=2,'expert'=4,'tile'=4] {'dp','expert'}, dimensions={0} | all-to-all | bytes 655360 | tf_op jit(solution)/shard_map/all_to_all | solution.py:60
  54.0 0.1 all_to_all.18
  54.1 14.2 %all_gather.15 = bf16[320,1024]{1,0:T(8,128)(2,1)} all-gather(bf16[160,1024]{1,0:T(8,128)(2,1)S(1)} %all_to_all.18), channel_id=1, replica_groups=mesh['dp'=2,'expert'=4,'tile'=4] {'dp'}, dimensions={0}, use_global_device_ids=true | all-gather | bytes 983040 | tf_op jit(solution)/shard_map/all_gather | solution.py:70
  68.3 0.0 all-gather.5.cloned.1.call-update
  68.3 0.0 all-gather.9.cloned.1.call-start
  68.3 0.0 all-gather.7.cloned.1.call-done
  68.4 0.7 all-gather.9.cloned.1.call-update
  69.0 19.8 %psum.7 = f32[4]{0:T(128)S(1)} all-reduce(f32[4]{0:T(128)S(1)} %get-tuple-element.2), channel_id=1, replica_groups=mesh['dp'=2,'expert'=4,'tile'=4] {'dp','expert'}, use_global_device_ids=true, to_apply=%region_4.5 | all-reduce | flops 4 | bytes 32 | tf_op jit(solution)/shard_map/psum | solution.py:63
  88.8 0.6 fusion.16
  90.1 3.6 %all-gather.5.cloned.1.call-done = bf16[320,4096]{1,0:T(8,128)(2,1)} async-done(((bf16[320,1024]{1,0:T(8,128)(2,1)}), bf16[320,4096]{1,0:T(8,128)(2,1)}) %all-gather.5.cloned.1.call-update) | async-done | bytes 2621456 | tf_op jit(solution)/shard_map/all_gather | solution.py:88
  93.7 7.3 %multiply_bitcast_fusion.1 = f32[1,1024,2048]{2,1,0:T(8,128)} fusion(bf16[320,1024]{1,0:T(8,128)(2,1)} %all_gather.15, f32[]{:T(128)S(6)} %div.27, bf16[320,4096]{1,0:T(8,128)(2,1)} %all-gather.5.cloned.1.call-done, s32[]{:T(128)S(6)} %select_n.54), kind=kOutput, calls=%fused_computation.1 | convolution fusion | flops 1344274432 | bytes 10354696 | tf_op jit(solution)/shard_map/dot_general | solution.py:13
  101.0 31.0 %all-gather.9.cloned.1.call-done = bf16[1280,1792]{1,0:T(8,128)(2,1)} async-done(((bf16[320,1792]{1,0:T(8,128)(2,1)}), bf16[1280,1792]{1,0:T(8,128)(2,1)}) %all-gather.9.cloned.1.call-update) | async-done | bytes 4587536 | tf_op jit(solution)/shard_map/all_gather | solution.py:89
  132.0 5.8 %copy.30 = bf16[4,320,1792]{2,0,1:T(4,128)(2,1)S(1)} copy(bf16[4,320,1792]{2,1,0:T(8,128)(2,1)} %bitcast.18) | data formatting | bytes 9175040 | tf_op jit(solution)/shard_map/all_gather | solution.py:89
  137.8 0.0 copy-start.1
  137.8 0.9 copy.31
  138.7 0.3 copy-done.1
  139.1 12.6 %multiply_bitcast_fusion = f32[1,1792,3584]{2,1,0:T(8,128)} fusion(bf16[320,1792]{1,0:T(8,128)(2,1)S(1)} %copy-done.1, f32[]{:T(128)S(6)} %div.27, bf16[320,7168]{1,0:T(8,128)(2,1)S(1)} %bitcast.17, s32[]{:T(128)S(6)} %select_n.58), kind=kOutput, calls=%fused_computation | convolution fusion | flops 4116840448 | bytes 29130760 | tf_op jit(solution)/shard_map/dot_general | solution.py:13
  (5 shorter events, 0.1 us)
Async XLA Ops:
  7.2 31.9 %copy-start = (bf16[64,1024]{1,0:T(8,128)(2,1)S(1)}, bf16[64,1024]{1,0:T(8,128)(2,1)}, u32[]{:S(2)}) copy-start(bf16[64,1024]{1,0:T(8,128)(2,1)} %param.4) | copy-start | bytes 393220
  7.2 12.6 %copy-start.2 = (s32[64,2]{0,1:T(2,128)S(1)}, s32[64,2]{0,1:T(2,128)}, u32[]{:S(2)}) copy-start(s32[64,2]{0,1:T(2,128)} %param.6) | copy-start | bytes 1540
  11.8 26.2 %all-to-all-start.1 = ((bf16[8,20,1792]{2,1,0:T(8,128)(2,1)}), bf16[8,20,1792]{2,1,0:T(8,128)(2,1)S(1)}, u32[]{:S(2)}, u32[]{:S(2)}) async-start(bf16[8,20,1792]{2,1,0:T(8,128)(2,1)} %all_to_all.19), calls=%async_computation.1 | async-start | bytes 1376256 | tf_op jit(solution)/shard_map/all_to_all | solution.py:61
  19.1 49.3 %all-gather.7.cloned.1.call-start = ((), (), s32[]{:S(2)}) async-start(), calls=%async_computation.3 | async-start | bytes 1720320 | tf_op jit(solution)/shard_map/all_gather | solution.py:71
  38.9 54.7 %all-gather.5.cloned.1.call-start = ((), (), s32[]{:S(2)}) async-start(), calls=%async_computation.2 | async-start | bytes 3276800 | tf_op jit(solution)/shard_map/all_gather | solution.py:88
  68.3 63.7 %all-gather.9.cloned.1.call-start = ((), (), s32[]{:S(2)}) async-start(), calls=%async_computation.4 | async-start | bytes 5734400 | tf_op jit(solution)/shard_map/all_gather | solution.py:89
  137.8 1.3 copy-start.1
Sparse Core Ops, SparseCore 0:
  39.0 28.0 all-gather.6
  68.7 24.8 all-gather.4
  95.2 36.6 all-gather.8
